TPU v7x, 8 devices: a whole 2x2x1 slice. The times are simulated.
8 devices in a mesh: bx: 2 (over z, y), sq: 4 (over x, core).
Axes of the slice: x: 2, y: 2, z: 1, core: 2. Of those that a mesh axis runs over, the one named last changes fastest.
Arguments:
- hidden: bfloat16 [128, 2048], P('bx'), parts along dimension 0
- w_query: bfloat16 [2048, 2048], P(None, 'sq')
- w_key: bfloat16 [2048, 128], replicated
- w_value: bfloat16 [2048, 128], replicated
- w_out: bfloat16 [2048, 2048], P('sq')
- k_cache: bfloat16 [128, 8192, 128], P('bx', 'sq'), parts along dimension 0
- v_cache: bfloat16 [128, 8192, 128], P('bx', 'sq'), parts along dimension 0
- lengths: int32 [128], P('bx'), parts along dimension 0
Outputs:
- output 1: bfloat16 [128, 2048], P('bx', 'sq'), parts along dimension 0
- output 2: bfloat16 [128, 128], P('bx'), parts along dimension 0
- output 3: bfloat16 [128, 128], P('bx'), parts along dimension 0
There are 2 independent parts. A program takes and returns all parts, laid end to end along the dimension named above; an argument that names none is the same for every part.
All inputs are finite; a program needn't handle non-finite values.
Results may differ from a plain program's by a relative error of at most 0.00560568.
Values sent between devices are 32-bit elements.
A program may use at most 1 GiB of HBM per device.

v0:
```python
import jax
import jax.numpy as jnp
from jax import lax
from jax.sharding import PartitionSpec as P

ROPE_BASE = 10000.0
NEG_BIG = -1e30


def rope_tables(lengths, head_dim):
    half_dim = head_dim // 2
    inv_freq = ROPE_BASE ** (-jnp.arange(half_dim, dtype=jnp.float32) * 2.0 / head_dim)
    angles = lengths.astype(jnp.float32)[:, None] * inv_freq[None, :]
    return jnp.cos(angles), jnp.sin(angles)


def apply_rope(x_val, cos_t, sin_t):
    half_dim = x_val.shape[-1] // 2
    x_low = x_val[..., :half_dim]
    x_high = x_val[..., half_dim:]
    return jnp.concatenate([x_low * cos_t - x_high * sin_t, x_high * cos_t + x_low * sin_t], axis=-1)


def solution(mesh):
    def local_step(hidden, w_query, w_key, w_value, w_out, k_cache, v_cache, lengths):
        num_rows = hidden.shape[0]
        head_dim = w_key.shape[1]
        local_heads = w_query.shape[1] // head_dim
        seq_local = k_cache.shape[1]
        shard_idx = lax.axis_index('sq')
        cos_t, sin_t = rope_tables(lengths, head_dim)
        q_proj = jnp.dot(hidden, w_query, preferred_element_type=jnp.float32).reshape(num_rows, local_heads, head_dim)
        k_new = apply_rope(jnp.dot(hidden, w_key, preferred_element_type=jnp.float32), cos_t, sin_t).astype(jnp.bfloat16)
        v_new = jnp.dot(hidden, w_value, preferred_element_type=jnp.float32).astype(jnp.bfloat16)
        q_gathered = lax.all_gather(q_proj, 'sq', axis=1, tiled=True)
        q_all = apply_rope(q_gathered, cos_t[:, None, :], sin_t[:, None, :]).astype(jnp.bfloat16)
        positions = shard_idx * seq_local + jnp.arange(seq_local)
        pos_hit = (positions[None, :] == lengths[:, None])[:, :, None]
        k_all = jnp.where(pos_hit, k_new[:, None, :], k_cache)
        v_all = jnp.where(pos_hit, v_new[:, None, :], v_cache)
        key_valid = positions[None, None, :] <= lengths[:, None, None]
        scores = jnp.einsum('bhd,bsd->bhs', q_all, k_all, preferred_element_type=jnp.float32) * (head_dim ** -0.5)
        scores = jnp.where(key_valid, scores, NEG_BIG)
        part_max = jnp.max(scores, axis=2)
        weights = jnp.where(key_valid, jnp.exp(scores - part_max[:, :, None]), 0.0)
        part_sum = jnp.sum(weights, axis=2)
        part_out = jnp.einsum('bhs,bsd->bhd', weights.astype(jnp.bfloat16), v_all, preferred_element_type=jnp.float32)
        glob_max = lax.pmax(part_max, 'sq')
        factor = jnp.exp(part_max - glob_max)
        out_sum = lax.psum_scatter(part_out * factor[:, :, None], 'sq', scatter_dimension=1, tiled=True)
        den_sum = lax.psum_scatter(part_sum * factor, 'sq', scatter_dimension=1, tiled=True)
        attn_out = (out_sum / den_sum[:, :, None]).astype(jnp.bfloat16).reshape(num_rows, local_heads * head_dim)
        y_part = jnp.dot(attn_out, w_out, preferred_element_type=jnp.float32)
        y_local = lax.psum_scatter(y_part, 'sq', scatter_dimension=1, tiled=True).astype(jnp.bfloat16)
        return y_local, k_new, v_new

    return jax.shard_map(
        local_step,
        mesh=mesh,
        in_specs=(P('bx', None), P(None, 'sq'), P(None, None), P(None, None), P('sq', None),
                  P('bx', 'sq', None), P('bx', 'sq', None), P('bx')),
        out_specs=(P('bx', 'sq'), P('bx', None), P('bx', None)),
        check_vma=False,
    )
```

profile of v0, /device:TPU:0, one launch (start us, length us, event | category | flops | bytes accessed | tf_op | source)
XLA Modules:
  0.0 145.6 jit_solution(13979742302834194896)
XLA Ops:
  7.2 0.8 convert_element_type.21
  8.0 1.3 fusion.35
  9.4 2.2 %convolution_bitcast_fusion = f32[8,4,8,128]{3,2,1,0:T(8,128)S(1)} fusion(bf16[64,2048]{1,0:T(8,128)(2,1)} %param.8, bf16[2048,512]{1,0:T(8,128)(2,1)} %param.9), kind=kOutput, calls=%fused_computation.19 | convolution fusion | flops 134217728 | bytes 2490368 | tf_op jit(solution)/shard_map/dot_general | solution.py:32
  11.6 11.9 %all_gather.3 = f32[64,16,128]{2,0,1:T(8,128)S(1)} all-gather(f32[64,4,128]{2,0,1:T(8,128)S(1)} %bitcast.22), channel_id=1, replica_groups=mesh['bx'=2,'sq'=4] {'sq'}, dimensions={1}, use_global_device_ids=true | all-gather | bytes 655360 | tf_op jit(solution)/shard_map/all_gather | solution.py:35
  23.4 0.2 fusion.34
  23.7 0.9 broadcast_compare_fusion.1
  24.6 0.2 multiply_cosine_fusion
  24.8 0.1 pad_maximum_fusion
  24.8 0.7 subtract_convert_fusion
  25.5 28.3 %fusion.8 = (f32[64,16]{1,0:T(8,128)S(1)}, f32[64,16,2048]{2,1,0:T(8,128)}) fusion(pred[64,2048]{1,0:T(8,128)(4,1)S(1)} %get-tuple-element.11, bf16[64,2048,128]{2,1,0:T(8,128)(2,1)} %param.13, pred[64,2048]{1,0:T(8,128)(4,1)S(1)} %get-tuple-element.12, bf16[64,128]{1,0:T(8,128)(2,1)S(1)} %pad_maximum_fusion, bf16[64,16,64]{2,1,0:T(8,128)(2,1)S(1)} %get-tuple-element.6, ...), kind=kOutput, calls=%fused_computation.10 | convolution fusion | flops 560462848 | bytes 42487808 | tf_op jit(solution)/shard_map/bhd,bsd->bhs/dot_general | solution.py:42
  53.8 10.4 %pmax.7 = f32[64,16]{1,0:T(8,128)S(1)} all-reduce(f32[64,16]{1,0:T(8,128)S(1)} %get-tuple-element.17), channel_id=1, replica_groups=mesh['bx'=2,'sq'=4] {'sq'}, use_global_device_ids=true, to_apply=%region_1.2 | all-reduce | flops 1024 | bytes 8192 | tf_op jit(solution)/shard_map/pmax | solution.py:48
  64.3 5.7 %fusion.9 = f32[64,16]{1,0:T(8,128)S(1)} fusion(f32[64,16,2048]{2,1,0:T(8,128)} %get-tuple-element.18, f32[64,16]{1,0:T(8,128)S(1)} %get-tuple-element.17, pred[64,2048]{1,0:T(8,128)(4,1)S(1)} %get-tuple-element.11), kind=kLoop, calls=%fused_computation.11 | loop fusion | flops 10484736 | bytes 8527872 | tf_op jit(solution)/shard_map/reduce_sum | solution.py:46
  69.9 0.2 convolution_convert_fusion
  70.2 31.2 %fusion.17 = f32[64,16,128]{2,1,0:T(8,128)S(1)} fusion(bf16[64,2048,128]{2,1,0:T(8,128)(2,1)} %param.14, pred[64,2048]{1,0:T(8,128)(4,1)S(1)} %get-tuple-element.12, bf16[64,128]{1,0:T(8,128)(2,1)S(1)} %convolution_convert_fusion, f32[64,16,2048]{2,1,0:T(8,128)S(1)} %copy-done.1, f32[64,16]{1,0:T(8,128)S(1)} %get-tuple-element.17, ...), kind=kOutput, calls=%fused_computation.18 | convolution fusion | flops 564264960 | bytes 42754048 | tf_op jit(solution)/shard_map/bhs,bsd->bhd/dot_general | solution.py:47
  101.4 0.9 copy.19
  102.4 0.0 reduce-scatter.6.cloned.1.call-start
  102.4 0.6 dynamic-slice
  103.7 10.6 %all-reduce = f32[64,16]{1,0:T(8,128)S(1)} all-reduce(f32[64,16]{1,0:T(8,128)S(1)} %get-tuple-element.3), channel_id=3, replica_groups=mesh['bx'=2,'sq'=4] {'sq'}, use_global_device_ids=true, to_apply=%region_4.5.clone | all-reduce | flops 1024 | bytes 8192
  114.3 0.1 constant_dynamic-slice_fusion
  114.4 0.1 copy.20
  114.4 4.3 %reduce-scatter.4.cloned.1.call-done = f32[64,4,128]{2,0,1:T(8,128)} async-done(((f32[64,16,128]{2,0,1:T(8,128)}), f32[64,4,128]{2,0,1:T(8,128)}) %reduce-scatter.4.cloned.1.call-update) | async-done | bytes 131088 | tf_op jit(solution)/shard_map/reduce_scatter | solution.py:50
  118.7 2.2 %fusion.25 = f32[64,2048]{1,0:T(8,128)} fusion(bf16[512,2048]{1,0:T(8,128)(2,1)S(1)} %copy-done, f32[64,4,128]{2,0,1:T(8,128)} %reduce-scatter.4.cloned.1.call-done, f32[64,4]{0,1:T(4,128)S(1)} %copy.20), kind=kOutput, calls=%fused_computation.30 | convolution fusion | flops 134283264 | bytes 2753536 | tf_op jit(solution)/shard_map/dot_general | solution.py:53
  120.9 16.3 %reduce-scatter.6.cloned.1.call-done = f32[64,512]{1,0:T(8,128)} async-done(((f32[64,2048]{1,0:T(8,128)}), f32[64,512]{1,0:T(8,128)}) %reduce-scatter.6.cloned.1.call-update) | async-done | bytes 131088 | tf_op jit(solution)/shard_map/reduce_scatter | solution.py:54
  137.2 1.5 %convert_element_type.25 = bf16[64,512]{1,0:T(8,128)(2,1)} convert(f32[64,512]{1,0:T(8,128)} %reduce-scatter.6.cloned.1.call-done) | non-fusion elementwise | flops 32768 | bytes 196608 | tf_op jit(solution)/shard_map/convert_element_type | solution.py:54
  (21 shorter events, 0.2 us)
Async XLA Ops:
  7.2 111.5 %copy-start = (bf16[512,2048]{1,0:T(8,128)(2,1)S(1)}, bf16[512,2048]{1,0:T(8,128)(2,1)}, u32[]{:S(2)}) copy-start(bf16[512,2048]{1,0:T(8,128)(2,1)} %param.12) | copy-start | bytes 6291460
  7.2 111.5 %reduce-scatter.4.cloned.1.call-start = ((), (), s32[]{:S(2)}) async-start(), calls=%async_computation.2 | async-start | bytes 655360 | tf_op jit(solution)/shard_map/reduce_scatter | solution.py:50
  24.8 29.0 %copy-start.4 = (bf16[64,128]{1,0:T(8,128)(2,1)}, bf16[64,128]{1,0:T(8,128)(2,1)S(1)}, u32[]{:S(2)}) copy-start(bf16[64,128]{1,0:T(8,128)(2,1)S(1)} %pad_maximum_fusion) | copy-start | bytes 49156
  53.8 16.1 %copy-start.2 = (bf16[64,2048]{1,0:T(8,128)(2,1)S(1)}, bf16[64,2048]{1,0:T(8,128)(2,1)}, u32[]{:S(2)}) copy-start(bf16[64,2048]{1,0:T(8,128)(2,1)} %param.8) | copy-start | bytes 786436
  53.8 16.1 %copy-start.3 = (bf16[2048,128]{1,0:T(8,128)(2,1)S(1)}, bf16[2048,128]{1,0:T(8,128)(2,1)}, u32[]{:S(2)}) copy-start(bf16[2048,128]{1,0:T(8,128)(2,1)} %param.11) | copy-start | bytes 1572868
  64.2 6.0 %copy-start.1 = (f32[64,16,2048]{2,1,0:T(8,128)S(1)}, f32[64,16,2048]{2,1,0:T(8,128)}, u32[]{:S(2)}) copy-start(f32[64,16,2048]{2,1,0:T(8,128)} %get-tuple-element.18) | copy-start | bytes 25165828
  70.2 31.2 %copy-start.5 = (bf16[64,128]{1,0:T(8,128)(2,1)}, bf16[64,128]{1,0:T(8,128)(2,1)S(1)}, u32[]{:S(2)}) copy-start(bf16[64,128]{1,0:T(8,128)(2,1)S(1)} %convolution_convert_fusion) | copy-start | bytes 49156
  70.2 32.2 %copy-start.6 = (u32[8]{0:T(128)S(1)}, u32[8]{0:T(128)}, u32[]{:S(2)}) copy-start(u32[8]{0:T(128)} %constant.23) | copy-start | bytes 100
  102.4 34.9 %reduce-scatter.6.cloned.1.call-start = ((), (), s32[]{:S(2)}) async-start(), calls=%async_computation.3 | async-start | bytes 655360 | tf_op jit(solution)/shard_map/reduce_scatter | solution.py:54
Sparse Core Ops, SparseCore 0:
  102.5 16.1 reduce-scatter.3
  121.2 16.0 reduce-scatter.5
where the time goes:
time: 146 us
  matrix products  65.4 us (45%)
  blocking collectives  32.9 us (23%)
  waiting for transfers between devices  20.6 us (14%)
  between operations  14.9 us (10%)
  other arithmetic  9.87 us (7%)
  local copies, waits for them, and re-layouts  1.95 us (1%)
    dot_general x1, matrix products, local_step(): jnp.einsum('bhs,bsd->bhd', weights.astype(jnp.bfloat16), v_all, preferred...  31.2 us
    dot_general x1, matrix products, local_step(): jnp.einsum('bhd,bsd->bhs', q_all, k_all, preferred_element_type=jnp.float32)  28.3 us
    reduce_scatter x1, waiting for transfers between devices, local_step(): lax.psum_scatter(y_part, 'sq', scatter_dimension=1, tiled=True)  16.3 us
    all_gather x1, blocking collectives, local_step(): q_gathered = lax.all_gather(q_proj, 'sq', axis=1, tiled=True)  11.9 us
    unnamed x1, blocking collectives  10.6 us
    pmax x1, blocking collectives, local_step(): glob_max = lax.pmax(part_max, 'sq')  10.4 us
    reduce_sum x1, other arithmetic, local_step(): part_sum = jnp.sum(weights, axis=2)  5.66 us
    reduce_scatter x1, waiting for transfers between devices, local_step(): lax.psum_scatter(part_out * factor[:, :, None], 'sq', scatter_dimension=1...  4.28 us
  transfers between devices with their start and end apart: 2, of which 2 were waited for; matrix products, arithmetic and copies ran while one was open for 1% of the time, Pallas kernels for 0%

commit v1 on v0

v1 whole, which is shorter than its diff:
```python
import math
import jax
import jax.numpy as jnp
from jax import lax
from jax.experimental import pallas as pl
from jax.experimental.pallas import tpu as pltpu
from jax.sharding import PartitionSpec as P

ROPE_BASE = 10000.0
GROUP = 8
RING = 3
CHUNK = 1024
TAIL_CHUNK = 512
MASKED = -3e38
MESH = pl.DeviceIdType.MESH
Y_BATCHES = {3: (0, 2), 5: (2, 2), 6: (4, 1)}


def make_kernel(rows, embed, seq, heads_local, hd):
    n_groups = rows // GROUP
    n_heads = 4 * heads_local
    assert n_heads * GROUP == hd and hd == 128
    q_cols = heads_local * hd
    last = n_groups - 1
    exp_c = hd ** -0.5 * math.log2(math.e)
    n_tail = seq // TAIL_CHUNK
    half = hd // 2
    freqs = [ROPE_BASE ** (-2.0 * i / hd) for i in range(half)]
    prow = heads_local * GROUP

    def kernel(hid_hbm, wq_hbm, wk_hbm, wv_hbm, wo_hbm, k_hbm, v_hbm, len_hbm,
               y_hbm, kn_hbm, vn_hbm,
               hid, wq, wkv, wo, lens_s, kb, vb, qrec, qmat, qblk, sbuf, oacc, mrow,
               knf, vnf, kn16, vn16, snew, psend, prec, attn, ysend, yrec, yout,
               in_sem, ksem, vsem, tsem, qs_sem, qr_sem, ps_sem, pr_sem, ys_sem, yr_sem, out_sem):
        bx = lax.axis_index('bx')
        me = lax.axis_index('sq')
        chip, core = me // 2, me % 2
        peers = [chip * 2 + (1 - core), (1 - chip) * 2 + core, (1 - chip) * 2 + (1 - core)]
        far_first = (1, 2, 0)
        base = me * seq

        def cp(src, dst, sem):
            return pltpu.make_async_copy(src, dst, sem)

        def k_copy(g):
            return cp(k_hbm.at[pl.ds(g * GROUP, GROUP)], kb.at[g % RING], ksem.at[g % RING])

        def v_copy(g):
            return cp(v_hbm.at[pl.ds(g * GROUP, GROUP)], vb.at[g % RING], vsem.at[g % RING])

        def v_tail(c):
            sl = slice(c * TAIL_CHUNK, (c + 1) * TAIL_CHUNK)
            return cp(v_hbm.at[last * GROUP:rows, sl, :], vb.at[last % RING, :, sl, :], tsem.at[c])

        ins = [cp(len_hbm, lens_s, in_sem.at[0]), cp(hid_hbm, hid, in_sem.at[1]), cp(wq_hbm, wq, in_sem.at[2]),
               cp(wk_hbm, wkv.at[0], in_sem.at[3]), cp(wv_hbm, wkv.at[1], in_sem.at[4]), cp(wo_hbm, wo, in_sem.at[5])]
        for c in ins[:5]:
            c.start()
        k_copy(0).start()
        k_copy(1).start()
        v_copy(0).start()

        barrier = pltpu.get_barrier_semaphore()
        for p in peers:
            pl.semaphore_signal(barrier, inc=1, device_id=(bx, p), device_id_type=MESH)

        k_copy(2).start()
        v_copy(1).start()
        ins[5].start()

        lane = lax.broadcasted_iota(jnp.int32, (1, hd), 1)
        lane_i = lane % half
        freq = jnp.zeros((1, hd), jnp.float32)
        for i in range(half):
            freq = jnp.where(lane_i == i, jnp.float32(freqs[i]), freq)
        ins[0].wait()
        sub = lax.broadcasted_iota(jnp.int32, (GROUP, 1), 0)
        pos_rows = []
        for g in range(n_groups):
            t = jnp.zeros((GROUP, 1), jnp.int32)
            for r in range(GROUP):
                t = jnp.where(sub == r, lens_s[g * GROUP + r], t)
            pos_rows.append(t)
        t_col = jnp.concatenate(pos_rows, axis=0).astype(jnp.float32)
        ang = t_col * freq
        cos_t = jnp.cos(ang)
        sin_t = jnp.where(lane < half, -1.0, 1.0) * jnp.sin(ang)

        def rope(x):
            return x * cos_t + pltpu.roll(x, half, 1) * sin_t

        ins[1].wait()
        ins[2].wait()
        qp = jnp.dot(hid[...], wq[...], preferred_element_type=jnp.float32)
        for h in range(heads_local):
            cs = slice(h * hd, (h + 1) * hd)
            qrec[me, :, cs] = rope(qp[:, cs]).astype(jnp.bfloat16).astype(jnp.float32)
        pl.semaphore_wait(barrier, 3)

        def q_copy(g, d):
            sl = pl.ds(g * GROUP, GROUP)
            return pltpu.make_async_remote_copy(
                src_ref=qrec.at[me, sl], dst_ref=qrec.at[me, sl], send_sem=qs_sem.at[d, g],
                recv_sem=qr_sem.at[d, g], device_id=(bx, peers[d]), device_id_type=MESH)

        for g in range(n_groups):
            for d in far_first:
                q_copy(g, d).start()

        ins[3].wait()
        ins[4].wait()
        kn = rope(jnp.dot(hid[...], wkv[0], preferred_element_type=jnp.float32)).astype(jnp.bfloat16)
        vn = jnp.dot(hid[...], wkv[1], preferred_element_type=jnp.float32).astype(jnp.bfloat16)
        kn16[...] = kn
        vn16[...] = vn
        cp(kn16, kn_hbm, out_sem.at[0]).start()
        cp(vn16, vn_hbm, out_sem.at[1]).start()
        knf = kn.astype(jnp.float32)
        vnf[...] = vn.astype(jnp.float32)
        for h in range(heads_local):
            s_h = jnp.sum(qrec[me, :, h * hd:(h + 1) * hd] * knf, axis=1, keepdims=True)
            snew[h] = jnp.broadcast_to(s_h, (rows, hd))

        lane_r = lane // n_heads

        def lens_row(g):
            out = jnp.zeros((1, hd), jnp.int32)
            for r in range(GROUP):
                out = jnp.where(lane_r == r, lens_s[g * GROUP + r], out)
            return out

        def q_wait(g):
            for d in range(3):
                q_copy(g, d).wait_recv()

        def build_q(g):
            for s in range(4):
                for h in range(heads_local):
                    qmat[pl.ds(s * heads_local + h, GROUP, stride=n_heads), :] = (
                        qrec[s, g * GROUP:(g + 1) * GROUP, h * hd:(h + 1) * hd])
            qt = qmat[...].T.astype(jnp.bfloat16)
            for r in range(GROUP):
                qblk[r * hd:(r + 1) * hd, :] = jnp.where(lane_r == r, qt, jnp.zeros_like(qt))

        def scores(g, c, ln):
            sl = slice(c * CHUNK, (c + 1) * CHUNK)
            kc = jnp.concatenate([kb[g % RING, r, sl, :] for r in range(GROUP)], axis=1)
            s = jnp.dot(kc, qblk[...], preferred_element_type=jnp.float32)
            pos = lax.broadcasted_iota(jnp.int32, (CHUNK, hd), 0) + (base + c * CHUNK)
            s = jnp.where(pos < ln, s, MASKED)
            sbuf[g % 2, sl, :] = s
            return jnp.max(s.reshape(CHUNK // 8, 8, hd), axis=0)

        def values(g, lo, size, mu):
            s = sbuf[g % 2, lo:lo + size, :]
            w = jnp.exp2((s - mu) * exp_c)
            part = jnp.sum(w.reshape(size // 8, 8, hd), axis=0)
            wt = w.astype(jnp.bfloat16).T
            for r in range(GROUP):
                rs = slice(r * n_heads, (r + 1) * n_heads)
                o = jnp.dot(wt[rs, :], vb[g % RING, r, lo:lo + size, :], preferred_element_type=jnp.float32)
                if lo == 0:
                    oacc[rs, :] = o
                else:
                    oacc[rs, :] += o
            return part

        def keep_max(g, m):
            mrow[g % 2] = jnp.broadcast_to(jnp.max(m, axis=0, keepdims=True), (8, hd))

        def p_copy(g, d):
            return pltpu.make_async_remote_copy(
                src_ref=psend.at[g, peers[d]], dst_ref=prec.at[d, g], send_sem=ps_sem.at[d, g],
                recv_sem=pr_sem.at[d, g], device_id=(bx, peers[d]), device_id_type=MESH)

        def send_part(g, l):
            for h in range(n_heads):
                k, hh = h // heads_local, h % heads_local
                psend[g, k, hh * GROUP:(hh + 1) * GROUP, :] = oacc[pl.ds(h, GROUP, stride=n_heads), :]
            l_row = jnp.sum(l, axis=0, keepdims=True)
            ml = jnp.where(sub == 0, mrow[g % 2], jnp.where(sub == 1, l_row, 0.0))
            for k in range(4):
                psend[g, k, prow:prow + 8, :] = ml
            for d in far_first:
                p_copy(g, d).start()

        prow_i = lax.broadcasted_iota(jnp.int32, (prow, hd), 0)
        pick = (prow_i % GROUP) * n_heads + me * heads_local + prow_i // GROUP
        lane_p = lax.broadcasted_iota(jnp.int32, (prow, hd), 1)
        picked = lane_p == pick

        def to_col(row):
            return jnp.sum(jnp.where(picked, row, 0.0), axis=1, keepdims=True)

        def combine(g):
            parts = [psend[g, me]] + [prec[d, g] for d in range(3)]
            rs = slice(g * GROUP, (g + 1) * GROUP)
            s_new = jnp.concatenate([snew[h, rs, :] for h in range(heads_local)], axis=0)
            ms = [to_col(p[prow:prow + 1, :]) for p in parts]
            ls = [to_col(p[prow + 1:prow + 2, :]) for p in parts]
            top = s_new
            for m in ms:
                top = jnp.maximum(top, m)
            f_new = jnp.exp2((s_new - top) * exp_c)
            den = f_new
            v_rows = vnf[rs, :]
            num = f_new * jnp.concatenate([v_rows] * heads_local, axis=0)
            for p, m, l in zip(parts, ms, ls):
                f = jnp.exp2((m - top) * exp_c)
                den = den + f * l
                num = num + f * p[:prow, :]
            o = num / den
            for h in range(heads_local):
                attn[rs, h * hd:(h + 1) * hd] = o[h * GROUP:(h + 1) * GROUP, :]

        def p_wait(g):
            for d in range(3):
                p_copy(g, d).wait_recv()

        y_batches = []

        def y_copy(b, g0, ng, d):
            sl = pl.ds(g0 * GROUP, ng * GROUP)
            return pltpu.make_async_remote_copy(
                src_ref=ysend.at[peers[d], sl], dst_ref=yrec.at[d, sl], send_sem=ys_sem.at[d, b],
                recv_sem=yr_sem.at[d, b], device_id=(bx, peers[d]), device_id_type=MESH)

        def project(g0, ng):
            b = len(y_batches)
            y_batches.append((b, g0, ng))
            sl = slice(g0 * GROUP, (g0 + ng) * GROUP)
            yp = jnp.dot(attn[sl, :].astype(jnp.bfloat16), wo[...], preferred_element_type=jnp.float32)
            for k in range(4):
                ysend[k, sl, :] = yp[:, k * q_cols:(k + 1) * q_cols]
            for d in far_first:
                y_copy(b, g0, ng, d).start()

        def finish(b, g0, ng):
            for d in range(3):
                y_copy(b, g0, ng, d).wait_recv()
            sl = slice(g0 * GROUP, (g0 + ng) * GROUP)
            yout[sl, :] = (ysend[me, sl, :] + yrec[0, sl, :] + yrec[1, sl, :] + yrec[2, sl, :]).astype(jnp.bfloat16)

        q_wait(0)
        build_q(0)
        k_copy(0).wait()
        ln = lens_row(0)
        m = jnp.full((8, hd), MASKED, jnp.float32)
        for c in range(seq // CHUNK):
            m = jnp.maximum(m, scores(0, c, ln))
        keep_max(0, m)

        def shift(g):
            return jnp.where(lens_row(g) > base, mrow[g % 2, 0:1, :], 0.0)

        for g in range(last):
            if g + 3 < n_groups:
                k_copy(g + 3).start()
            if g + 2 < last:
                v_copy(g + 2).start()
            if g + 2 == last:
                for c in range(n_tail):
                    v_tail(c).start()
            q_wait(g + 1)
            if g >= 2:
                p_wait(g - 2)
            if g == 3:
                ins[5].wait()
            k_copy(g + 1).wait()
            v_copy(g).wait()
            build_q(g + 1)
            mu = shift(g)
            ln = lens_row(g + 1)
            m = jnp.full((8, hd), MASKED, jnp.float32)
            l = jnp.zeros((8, hd), jnp.float32)
            for c in range(seq // CHUNK):
                l = l + values(g, c * CHUNK, CHUNK, mu)
                m = jnp.maximum(m, scores(g + 1, c, ln))
            keep_max(g + 1, m)
            send_part(g, l)
            if g >= 2:
                combine(g - 2)
            if g in Y_BATCHES:
                project(*Y_BATCHES[g])

        mu = shift(last)
        l = jnp.zeros((8, hd), jnp.float32)
        for c in range(n_tail):
            v_tail(c).wait()
            l = l + values(last, c * TAIL_CHUNK, TAIL_CHUNK, mu)
        send_part(last, l)
        p_wait(last - 2)
        combine(last - 2)
        p_wait(last - 1)
        combine(last - 1)
        project(last - 2, 2)
        for b in y_batches[:-1]:
            finish(*b)
        p_wait(last)
        combine(last)
        project(last, 1)
        finish(*y_batches[-2])
        finish(*y_batches[-1])
        y_out = cp(yout, y_hbm, out_sem.at[2])
        y_out.start()
        for g in range(n_groups):
            for d in range(3):
                q_copy(g, d).wait_send()
                p_copy(g, d).wait_send()
        for b in y_batches:
            for d in range(3):
                y_copy(*b, d).wait_send()
        cp(kn16, kn_hbm, out_sem.at[0]).wait()
        cp(vn16, vn_hbm, out_sem.at[1]).wait()
        y_out.wait()

    f32, bf16 = jnp.float32, jnp.bfloat16
    dma = pltpu.SemaphoreType.DMA
    n_b = len(Y_BATCHES) + 2
    scratch = [
        pltpu.VMEM((rows, embed), bf16), pltpu.VMEM((embed, q_cols), bf16), pltpu.VMEM((2, embed, hd), bf16),
        pltpu.VMEM((q_cols, embed), bf16), pltpu.SMEM((rows,), jnp.int32),
        pltpu.VMEM((RING, GROUP, seq, hd), bf16), pltpu.VMEM((RING, GROUP, seq, hd), bf16),
        pltpu.VMEM((4, rows, q_cols), f32), pltpu.VMEM((hd, hd), f32), pltpu.VMEM((GROUP * hd, hd), bf16),
        pltpu.VMEM((2, seq, hd), f32), pltpu.VMEM((hd, hd), f32), pltpu.VMEM((2, 8, hd), f32),
        pltpu.VMEM((rows, hd), f32), pltpu.VMEM((rows, hd), f32),
        pltpu.VMEM((rows, hd), bf16), pltpu.VMEM((rows, hd), bf16), pltpu.VMEM((heads_local, rows, hd), f32),
        pltpu.VMEM((n_groups, 4, prow + 8, hd), f32), pltpu.VMEM((3, n_groups, prow + 8, hd), f32),
        pltpu.VMEM((rows, q_cols), f32), pltpu.VMEM((4, rows, q_cols), f32), pltpu.VMEM((3, rows, q_cols), f32),
        pltpu.VMEM((rows, q_cols), bf16),
        dma((6,)), dma((RING,)), dma((RING,)), dma((n_tail,)), dma((3, n_groups)), dma((3, n_groups)),
        dma((3, n_groups)), dma((3, n_groups)), dma((3, n_b)), dma((3, n_b)), dma((3,)),
    ]
    return kernel, scratch


def solution(mesh):
    def local_step(hidden, w_query, w_key, w_value, w_out, k_cache, v_cache, lengths):
        rows, embed = hidden.shape
        hd = w_key.shape[1]
        seq = k_cache.shape[1]
        heads_local = w_query.shape[1] // hd
        q_cols = heads_local * hd
        kernel, scratch = make_kernel(rows, embed, seq, heads_local, hd)
        any_spec = pl.BlockSpec(memory_space=pl.ANY)
        return pl.pallas_call(
            kernel,
            out_shape=(jax.ShapeDtypeStruct((rows, q_cols), jnp.bfloat16),
                       jax.ShapeDtypeStruct((rows, hd), jnp.bfloat16),
                       jax.ShapeDtypeStruct((rows, hd), jnp.bfloat16)),
            in_specs=[any_spec] * 8,
            out_specs=(any_spec,) * 3,
            scratch_shapes=scratch,
            compiler_params=pltpu.CompilerParams(
                collective_id=0, has_side_effects=True, vmem_limit_bytes=67043328),
            name="mqa_decode",
        )(hidden, w_query, w_key, w_value, w_out, k_cache, v_cache, lengths)

    return jax.shard_map(
        local_step,
        mesh=mesh,
        in_specs=(P('bx', None), P(None, 'sq'), P(None, None), P(None, None), P('sq', None),
                  P('bx', 'sq', None), P('bx', 'sq', None), P('bx')),
        out_specs=(P('bx', 'sq'), P('bx', None), P('bx', None)),
        check_vma=False,
    )
```

time: 146 us -> 42.1 us (0.29)
  matrix products: 65.4 us -> 0 us
  Pallas kernels: 0 us -> 37.1 us
  blocking collectives: 32.9 us -> 0 us
  waiting for transfers between devices: 20.6 us -> 0 us
  between operations: 14.9 us -> 0.64 us
  other arithmetic: 9.87 us -> 0 us
  local copies, waits for them, and re-layouts: 1.95 us -> 4.12 us
    dot_general x6 -> x0, matrix products: 65.4 us -> none  [the longest x1 31.2 us: local_step(): jnp.einsum('bhs,bsd->bhd', weights.astype(jnp.bfloat16), v_all, preferred...]
    pallas_call x0 -> x1, Pallas kernels: none -> 37.1 us  [local_step(): pl.pallas_call(kernel, out_shape=(jax.ShapeDtypeStruct((rows, q_cols), jn...]
    reduce_scatter x2 -> x0, waiting for transfers between devices: 20.6 us -> none  [the longest x1 16.3 us: local_step(): lax.psum_scatter(y_part, 'sq', scatter_dimension=1, tiled=True)]
    all_gather x1 -> x0, blocking collectives: 11.9 us -> none  [local_step(): q_gathered = lax.all_gather(q_proj, 'sq', axis=1, tiled=True)]
    unnamed x1 -> x0, blocking collectives: 10.6 us -> none
    pmax x1 -> x0, blocking collectives: 10.4 us -> none  [local_step(): glob_max = lax.pmax(part_max, 'sq')]
    reduce_sum x1 -> x0, other arithmetic: 5.66 us -> none  [local_step(): part_sum = jnp.sum(weights, axis=2)]
    unnamed x16 -> x3, local copies, waits for them, and re-layouts: 0.71 us -> 4.12 us
  transfers between devices with their start and end apart: 2 -> 0, of which waited for: 2 -> 0; matrix products, arithmetic and copies ran while one was open for 1% -> 0% of each run, Pallas kernels for 0% -> 0%
where the time goes in v1:
time: 42.1 us; the launch traced here: 41.8 us
  Pallas kernels  37.1 us (88%)
  local copies, waits for them, and re-layouts  4.12 us (10%)
  between operations  0.64 us (2%)
    pallas_call x1, Pallas kernels, local_step(): pl.pallas_call(kernel, out_shape=(jax.ShapeDtypeStruct((rows, q_cols), jn...  37.1 us
    unnamed x3, local copies, waits for them, and re-layouts  4.12 us

profile of v1, /device:TPU:0, one launch (start us, length us, event | category | flops | bytes accessed | tf_op | source)
XLA Modules:
  0.0 41.8 jit_solution(4394704048056660956)
XLA Ops:
  0.6 37.1 %mqa_decode.1 = (bf16[64,512]{1,0:T(8,128)(2,1)}, bf16[64,128]{1,0:T(8,128)(2,1)}, bf16[64,128]{1,0:T(8,128)(2,1)}) custom-call(bf16[64,2048]{1,0:T(8,128)(2,1)} %hid_hbm.1, bf16[2048,512]{1,0:T(8,128)(2,1)} %wq_hbm.1, bf16[2048,128]{1,0:T(8,128)(2,1)} %wk_hbm.1, bf16[2048,128]{1,0:T(8,128)(2,1)} %wv_hbm.1, bf16[512,2048]{1,0:T(8,128)(2,1)} %wo_hbm.1, ...), custom_call_target="tpu_custom_call" | custom-call | tf_op jit(solution)/shard_map/mqa_decode/pallas_call | solution.py:347
  37.7 1.5 %copy.14 = bf16[64,512]{1,0:T(8,128)(2,1)} copy(bf16[64,512]{1,0:T(8,128)(2,1)} %get-tuple-element.6) | data formatting | bytes 131072
  39.2 1.3 %copy.15 = bf16[64,128]{1,0:T(8,128)(2,1)} copy(bf16[64,128]{1,0:T(8,128)(2,1)} %get-tuple-element.7) | data formatting | bytes 32768
  40.5 1.3 %copy.16 = bf16[64,128]{1,0:T(8,128)(2,1)} copy(bf16[64,128]{1,0:T(8,128)(2,1)} %get-tuple-element.8) | data formatting | bytes 32768

commit v2 on v1

--- a/solution.py
+++ b/solution.py
@@ -30,8 +30,8 @@
 
     def kernel(hid_hbm, wq_hbm, wk_hbm, wv_hbm, wo_hbm, k_hbm, v_hbm, len_hbm,
                y_hbm, kn_hbm, vn_hbm,
-               hid, wq, wkv, wo, lens_s, kb, vb, qrec, qmat, qblk, sbuf, oacc, mrow,
-               knf, vnf, kn16, vn16, snew, psend, prec, attn, ysend, yrec, yout,
+               hid, wq, wkv, wo, lens_s, kb, vb, qown, qrec, qmat, qblk, sbuf, oacc, mrow,
+               vnf, kn16, vn16, snew, psend, prec, attn, ysend, yrec, yout,
                in_sem, ksem, vsem, tsem, qs_sem, qr_sem, ps_sem, pr_sem, ys_sem, yr_sem, out_sem):
         bx = lax.axis_index('bx')
         me = lax.axis_index('sq')
@@ -95,14 +95,14 @@
         qp = jnp.dot(hid[...], wq[...], preferred_element_type=jnp.float32)
         for h in range(heads_local):
             cs = slice(h * hd, (h + 1) * hd)
-            qrec[me, :, cs] = rope(qp[:, cs]).astype(jnp.bfloat16).astype(jnp.float32)
+            q_h = rope(qp[:, cs]).astype(jnp.bfloat16).astype(jnp.float32)
+            qown[:, :, cs] = q_h.reshape(n_groups, GROUP, hd)
         pl.semaphore_wait(barrier, 3)
 
         def q_copy(g, d):
-            sl = pl.ds(g * GROUP, GROUP)
             return pltpu.make_async_remote_copy(
-                src_ref=qrec.at[me, sl], dst_ref=qrec.at[me, sl], send_sem=qs_sem.at[d, g],
-                recv_sem=qr_sem.at[d, g], device_id=(bx, peers[d]), device_id_type=MESH)
+                src_ref=qown.at[g], dst_ref=qrec.at[g, d], send_sem=qs_sem.at[d],
+                recv_sem=qr_sem.at[g], device_id=(bx, peers[d]), device_id_type=MESH)
 
         for g in range(n_groups):
             for d in far_first:
@@ -119,7 +119,8 @@
         knf = kn.astype(jnp.float32)
         vnf[...] = vn.astype(jnp.float32)
         for h in range(heads_local):
-            s_h = jnp.sum(qrec[me, :, h * hd:(h + 1) * hd] * knf, axis=1, keepdims=True)
+            q_h = qown[:, :, h * hd:(h + 1) * hd].reshape(rows, hd)
+            s_h = jnp.sum(q_h * knf, axis=1, keepdims=True)
             snew[h] = jnp.broadcast_to(s_h, (rows, hd))
 
         lane_r = lane // n_heads
@@ -131,14 +132,14 @@
             return out
 
         def q_wait(g):
-            for d in range(3):
-                q_copy(g, d).wait_recv()
+            pltpu.make_async_copy(qrec.at[g], qrec.at[g], qr_sem.at[g]).wait()
 
         def build_q(g):
             for s in range(4):
                 for h in range(heads_local):
-                    qmat[pl.ds(s * heads_local + h, GROUP, stride=n_heads), :] = (
-                        qrec[s, g * GROUP:(g + 1) * GROUP, h * hd:(h + 1) * hd])
+                    cs = slice(h * hd, (h + 1) * hd)
+                    blk = qown[g, :, cs] if s == 3 else qrec[g, s, :, cs]
+                    qmat[pl.ds(s * heads_local + h, GROUP, stride=n_heads), :] = blk
             qt = qmat[...].T.astype(jnp.bfloat16)
             for r in range(GROUP):
                 qblk[r * hd:(r + 1) * hd, :] = jnp.where(lane_r == r, qt, jnp.zeros_like(qt))
@@ -157,9 +158,11 @@
             w = jnp.exp2((s - mu) * exp_c)
             part = jnp.sum(w.reshape(size // 8, 8, hd), axis=0)
             wt = w.astype(jnp.bfloat16).T
-            for r in range(GROUP):
-                rs = slice(r * n_heads, (r + 1) * n_heads)
-                o = jnp.dot(wt[rs, :], vb[g % RING, r, lo:lo + size, :], preferred_element_type=jnp.float32)
+            for r in range(0, GROUP, 2):
+                rs = slice(r * n_heads, (r + 2) * n_heads)
+                vc = jnp.concatenate([vb[g % RING, r + i, lo:lo + size, :] for i in range(2)], axis=1)
+                o = jnp.dot(wt[rs, :], vc, preferred_element_type=jnp.float32)
+                o = jnp.concatenate([o[:n_heads, :hd], o[n_heads:, hd:]], axis=0)
                 if lo == 0:
                     oacc[rs, :] = o
                 else:
@@ -171,34 +174,34 @@
 
         def p_copy(g, d):
             return pltpu.make_async_remote_copy(
-                src_ref=psend.at[g, peers[d]], dst_ref=prec.at[d, g], send_sem=ps_sem.at[d, g],
-                recv_sem=pr_sem.at[d, g], device_id=(bx, peers[d]), device_id_type=MESH)
+                src_ref=psend.at[d, g], dst_ref=prec.at[g, d], send_sem=ps_sem.at[d],
+                recv_sem=pr_sem.at[g], device_id=(bx, peers[d]), device_id_type=MESH)
 
         def send_part(g, l):
             for h in range(n_heads):
                 k, hh = h // heads_local, h % heads_local
-                psend[g, k, hh * GROUP:(hh + 1) * GROUP, :] = oacc[pl.ds(h, GROUP, stride=n_heads), :]
+                psend[k, g, hh * GROUP:(hh + 1) * GROUP, :] = oacc[pl.ds(h, GROUP, stride=n_heads), :]
             l_row = jnp.sum(l, axis=0, keepdims=True)
             ml = jnp.where(sub == 0, mrow[g % 2], jnp.where(sub == 1, l_row, 0.0))
             for k in range(4):
-                psend[g, k, prow:prow + 8, :] = ml
+                psend[k, g, prow:prow + 8, :] = ml
             for d in far_first:
                 p_copy(g, d).start()
 
         prow_i = lax.broadcasted_iota(jnp.int32, (prow, hd), 0)
-        pick = (prow_i % GROUP) * n_heads + me * heads_local + prow_i // GROUP
+        pick = (prow_i % GROUP) * n_heads + prow_i // GROUP
         lane_p = lax.broadcasted_iota(jnp.int32, (prow, hd), 1)
-        picked = lane_p == pick
-
-        def to_col(row):
-            return jnp.sum(jnp.where(picked, row, 0.0), axis=1, keepdims=True)
+        picked = [lane_p == pick + d * heads_local for d in range(4)]
+
+        def to_col(d, row):
+            return jnp.sum(jnp.where(picked[d], row, 0.0), axis=1, keepdims=True)
 
         def combine(g):
-            parts = [psend[g, me]] + [prec[d, g] for d in range(3)]
+            parts = [prec[g, d] for d in range(3)] + [psend[3, g]]
             rs = slice(g * GROUP, (g + 1) * GROUP)
             s_new = jnp.concatenate([snew[h, rs, :] for h in range(heads_local)], axis=0)
-            ms = [to_col(p[prow:prow + 1, :]) for p in parts]
-            ls = [to_col(p[prow + 1:prow + 2, :]) for p in parts]
+            ms = [to_col(d, p[prow:prow + 1, :]) for d, p in enumerate(parts)]
+            ls = [to_col(d, p[prow + 1:prow + 2, :]) for d, p in enumerate(parts)]
             top = s_new
             for m in ms:
                 top = jnp.maximum(top, m)
@@ -215,16 +218,15 @@
                 attn[rs, h * hd:(h + 1) * hd] = o[h * GROUP:(h + 1) * GROUP, :]
 
         def p_wait(g):
-            for d in range(3):
-                p_copy(g, d).wait_recv()
+            pltpu.make_async_copy(prec.at[g], prec.at[g], pr_sem.at[g]).wait()
 
         y_batches = []
 
         def y_copy(b, g0, ng, d):
             sl = pl.ds(g0 * GROUP, ng * GROUP)
             return pltpu.make_async_remote_copy(
-                src_ref=ysend.at[peers[d], sl], dst_ref=yrec.at[d, sl], send_sem=ys_sem.at[d, b],
-                recv_sem=yr_sem.at[d, b], device_id=(bx, peers[d]), device_id_type=MESH)
+                src_ref=ysend.at[peers[d], sl], dst_ref=yrec.at[d, sl], send_sem=ys_sem.at[d],
+                recv_sem=yr_sem.at[b], device_id=(bx, peers[d]), device_id_type=MESH)
 
         def project(g0, ng):
             b = len(y_batches)
@@ -237,9 +239,8 @@
                 y_copy(b, g0, ng, d).start()
 
         def finish(b, g0, ng):
-            for d in range(3):
-                y_copy(b, g0, ng, d).wait_recv()
             sl = slice(g0 * GROUP, (g0 + ng) * GROUP)
+            pltpu.make_async_copy(yrec.at[:, sl], yrec.at[:, sl], yr_sem.at[b]).wait()
             yout[sl, :] = (ysend[me, sl, :] + yrec[0, sl, :] + yrec[1, sl, :] + yrec[2, sl, :]).astype(jnp.bfloat16)
 
         q_wait(0)
@@ -304,13 +305,10 @@
         finish(*y_batches[-1])
         y_out = cp(yout, y_hbm, out_sem.at[2])
         y_out.start()
-        for g in range(n_groups):
-            for d in range(3):
-                q_copy(g, d).wait_send()
-                p_copy(g, d).wait_send()
-        for b in y_batches:
-            for d in range(3):
-                y_copy(*b, d).wait_send()
+        for d in range(3):
+            pltpu.make_async_copy(qown, qown, qs_sem.at[d]).wait()
+            pltpu.make_async_copy(psend.at[d], psend.at[d], ps_sem.at[d]).wait()
+            pltpu.make_async_copy(ysend.at[d], ysend.at[d], ys_sem.at[d]).wait()
         cp(kn16, kn_hbm, out_sem.at[0]).wait()
         cp(vn16, vn_hbm, out_sem.at[1]).wait()
         y_out.wait()
@@ -322,17 +320,31 @@
         pltpu.VMEM((rows, embed), bf16), pltpu.VMEM((embed, q_cols), bf16), pltpu.VMEM((2, embed, hd), bf16),
         pltpu.VMEM((q_cols, embed), bf16), pltpu.SMEM((rows,), jnp.int32),
         pltpu.VMEM((RING, GROUP, seq, hd), bf16), pltpu.VMEM((RING, GROUP, seq, hd), bf16),
-        pltpu.VMEM((4, rows, q_cols), f32), pltpu.VMEM((hd, hd), f32), pltpu.VMEM((GROUP * hd, hd), bf16),
+        pltpu.VMEM((n_groups, GROUP, q_cols), f32), pltpu.VMEM((n_groups, 3, GROUP, q_cols), f32),
+        pltpu.VMEM((hd, hd), f32), pltpu.VMEM((GROUP * hd, hd), bf16),
         pltpu.VMEM((2, seq, hd), f32), pltpu.VMEM((hd, hd), f32), pltpu.VMEM((2, 8, hd), f32),
-        pltpu.VMEM((rows, hd), f32), pltpu.VMEM((rows, hd), f32),
+        pltpu.VMEM((rows, hd), f32),
         pltpu.VMEM((rows, hd), bf16), pltpu.VMEM((rows, hd), bf16), pltpu.VMEM((heads_local, rows, hd), f32),
-        pltpu.VMEM((n_groups, 4, prow + 8, hd), f32), pltpu.VMEM((3, n_groups, prow + 8, hd), f32),
+        pltpu.VMEM((4, n_groups, prow + 8, hd), f32), pltpu.VMEM((n_groups, 3, prow + 8, hd), f32),
         pltpu.VMEM((rows, q_cols), f32), pltpu.VMEM((4, rows, q_cols), f32), pltpu.VMEM((3, rows, q_cols), f32),
         pltpu.VMEM((rows, q_cols), bf16),
-        dma((6,)), dma((RING,)), dma((RING,)), dma((n_tail,)), dma((3, n_groups)), dma((3, n_groups)),
-        dma((3, n_groups)), dma((3, n_groups)), dma((3, n_b)), dma((3, n_b)), dma((3,)),
+        dma((6,)), dma((RING,)), dma((RING,)), dma((n_tail,)), dma((3,)), dma((n_groups,)),
+        dma((3,)), dma((n_groups,)), dma((3,)), dma((n_b,)), dma((3,)),
     ]
     return kernel, scratch
+
+
+def store_kernel(y_ref, k_ref, v_ref, yo_ref, ko_ref, vo_ref, y_buf, k_buf, v_buf, sem):
+    trips = [(y_ref, y_buf, yo_ref), (k_ref, k_buf, ko_ref), (v_ref, v_buf, vo_ref)]
+    reads = [pltpu.make_async_copy(a, b, sem.at[i]) for i, (a, b, _) in enumerate(trips)]
+    writes = [pltpu.make_async_copy(b, c, sem.at[3 + i]) for i, (_, b, c) in enumerate(trips)]
+    for c in reads:
+        c.start()
+    for r, w in zip(reads, writes):
+        r.wait()
+        w.start()
+    for w in writes:
+        w.wait()
 
 
 def solution(mesh):
@@ -344,11 +356,12 @@
         q_cols = heads_local * hd
         kernel, scratch = make_kernel(rows, embed, seq, heads_local, hd)
         any_spec = pl.BlockSpec(memory_space=pl.ANY)
-        return pl.pallas_call(
+        outs = (jax.ShapeDtypeStruct((rows, q_cols), jnp.bfloat16),
+                jax.ShapeDtypeStruct((rows, hd), jnp.bfloat16),
+                jax.ShapeDtypeStruct((rows, hd), jnp.bfloat16))
+        raw = pl.pallas_call(
             kernel,
-            out_shape=(jax.ShapeDtypeStruct((rows, q_cols), jnp.bfloat16),
-                       jax.ShapeDtypeStruct((rows, hd), jnp.bfloat16),
-                       jax.ShapeDtypeStruct((rows, hd), jnp.bfloat16)),
+            out_shape=outs,
             in_specs=[any_spec] * 8,
             out_specs=(any_spec,) * 3,
             scratch_shapes=scratch,
@@ -356,6 +369,14 @@
                 collective_id=0, has_side_effects=True, vmem_limit_bytes=67043328),
             name="mqa_decode",
         )(hidden, w_query, w_key, w_value, w_out, k_cache, v_cache, lengths)
+        return pl.pallas_call(
+            store_kernel,
+            out_shape=outs,
+            in_specs=[any_spec] * 3,
+            out_specs=(any_spec,) * 3,
+            scratch_shapes=[pltpu.VMEM(o.shape, o.dtype) for o in outs] + [pltpu.SemaphoreType.DMA((6,))],
+            name="store_outputs",
+        )(*raw)
 
     return jax.shard_map(
         local_step,

time: 42.1 us -> 36.4 us (0.86)
  local copies, waits for them, and re-layouts: 4.12 us -> 0 us
  Pallas kernels: 37.1 us -> 35.5 us
    unnamed x3 -> x0, local copies, waits for them, and re-layouts: 4.12 us -> none
    pallas_call x1 -> x2, Pallas kernels: 37.1 us -> 35.5 us  [the longest x1 33.9 us: local_step(): pl.pallas_call(kernel, out_shape=outs, in_specs=[any_spec] * 8, out_specs...]
where the time goes in v2:
time: 36.4 us; the launch traced here: 36.3 us
  Pallas kernels  35.5 us (98%)
  between operations  0.8 us (2%)
    pallas_call x1, Pallas kernels, local_step(): pl.pallas_call(kernel, out_shape=outs, in_specs=[any_spec] * 8, out_specs...  33.9 us
    pallas_call x1, Pallas kernels, local_step(): pl.pallas_call(store_kernel, out_shape=outs, in_specs=[any_spec] * 3, out...  1.53 us

profile of v2, /device:TPU:0, one launch (start us, length us, event | category | flops | bytes accessed | tf_op | source)
XLA Modules:
  0.0 36.3 jit_solution(10336821703564881440)
XLA Ops:
  0.6 33.9 %mqa_decode.1 = (bf16[64,512]{1,0:T(8,128)(2,1)}, bf16[64,128]{1,0:T(8,128)(2,1)}, bf16[64,128]{1,0:T(8,128)(2,1)}) custom-call(bf16[64,2048]{1,0:T(8,128)(2,1)} %hid_hbm.1, bf16[2048,512]{1,0:T(8,128)(2,1)} %wq_hbm.1, bf16[2048,128]{1,0:T(8,128)(2,1)} %wk_hbm.1, bf16[2048,128]{1,0:T(8,128)(2,1)} %wv_hbm.1, bf16[512,2048]{1,0:T(8,128)(2,1)} %wo_hbm.1, ...), custom_call_target="tpu_custom_call" | custom-call | tf_op jit(solution)/shard_map/mqa_decode/pallas_call | solution.py:362
  34.6 1.5 %store_outputs.1 = (bf16[64,512]{1,0:T(8,128)(2,1)}, bf16[64,128]{1,0:T(8,128)(2,1)}, bf16[64,128]{1,0:T(8,128)(2,1)}) custom-call(bf16[64,512]{1,0:T(8,128)(2,1)} %get-tuple-element.6.y_ref, bf16[64,128]{1,0:T(8,128)(2,1)} %get-tuple-element.7.k_ref, bf16[64,128]{1,0:T(8,128)(2,1)} %get-tuple-element.8.v_ref), custom_call_target="tpu_custom_call" | custom-call | tf_op jit(solution)/shard_map/store_outputs/pallas_call | solution.py:372

commit v3 on v2

--- a/solution.py
+++ b/solution.py
@@ -10,10 +10,10 @@
 GROUP = 8
 RING = 3
 CHUNK = 1024
-TAIL_CHUNK = 512
+PIECE = 4
 MASKED = -3e38
 MESH = pl.DeviceIdType.MESH
-Y_BATCHES = {3: (0, 2), 5: (2, 2), 6: (4, 1)}
+Y_BATCHES = {3: (0, 2), 5: (2, 2)}
 
 
 def make_kernel(rows, embed, seq, heads_local, hd):
@@ -23,7 +23,8 @@
     q_cols = heads_local * hd
     last = n_groups - 1
     exp_c = hd ** -0.5 * math.log2(math.e)
-    n_tail = seq // TAIL_CHUNK
+    n_pieces = GROUP // PIECE
+    piece_rows = heads_local * PIECE
     half = hd // 2
     freqs = [ROPE_BASE ** (-2.0 * i / hd) for i in range(half)]
     prow = heads_local * GROUP
@@ -31,8 +32,9 @@
     def kernel(hid_hbm, wq_hbm, wk_hbm, wv_hbm, wo_hbm, k_hbm, v_hbm, len_hbm,
                y_hbm, kn_hbm, vn_hbm,
                hid, wq, wkv, wo, lens_s, kb, vb, qown, qrec, qmat, qblk, sbuf, oacc, mrow,
-               vnf, kn16, vn16, snew, psend, prec, attn, ysend, yrec, yout,
-               in_sem, ksem, vsem, tsem, qs_sem, qr_sem, ps_sem, pr_sem, ys_sem, yr_sem, out_sem):
+               vnf, kn16, vn16, snew, wts, psend, prec, tsend, trec, attn, ysend,
+               in_sem, ksem, vsem, tsem, qs_sem, qr_sem, ps_sem, pr_sem, ts_sem, tr_sem, ys_sem, yr_sem,
+               out_sem):
         bx = lax.axis_index('bx')
         me = lax.axis_index('sq')
         chip, core = me // 2, me % 2
@@ -50,8 +52,8 @@
             return cp(v_hbm.at[pl.ds(g * GROUP, GROUP)], vb.at[g % RING], vsem.at[g % RING])
 
         def v_tail(c):
-            sl = slice(c * TAIL_CHUNK, (c + 1) * TAIL_CHUNK)
-            return cp(v_hbm.at[last * GROUP:rows, sl, :], vb.at[last % RING, :, sl, :], tsem.at[c])
+            r0 = last * GROUP + c * PIECE
+            return cp(v_hbm.at[r0:r0 + PIECE], vb.at[last % RING, c * PIECE:(c + 1) * PIECE], tsem.at[c])
 
         ins = [cp(len_hbm, lens_s, in_sem.at[0]), cp(hid_hbm, hid, in_sem.at[1]), cp(wq_hbm, wq, in_sem.at[2]),
                cp(wk_hbm, wkv.at[0], in_sem.at[3]), cp(wv_hbm, wkv.at[1], in_sem.at[4]), cp(wo_hbm, wo, in_sem.at[5])]
@@ -153,16 +155,21 @@
             sbuf[g % 2, sl, :] = s
             return jnp.max(s.reshape(CHUNK // 8, 8, hd), axis=0)
 
+        def weights(g, lo, size, mu):
+            w = jnp.exp2((sbuf[g % 2, lo:lo + size, :] - mu) * exp_c)
+            part = jnp.sum(w.reshape(size // 8, 8, hd), axis=0)
+            return w.astype(jnp.bfloat16).T, part
+
+        def weighted(g, r, wt, lo, size):
+            vc = jnp.concatenate([vb[g % RING, r + i, lo:lo + size, :] for i in range(2)], axis=1)
+            o = jnp.dot(wt, vc, preferred_element_type=jnp.float32)
+            return jnp.concatenate([o[:n_heads, :hd], o[n_heads:, hd:]], axis=0)
+
         def values(g, lo, size, mu):
-            s = sbuf[g % 2, lo:lo + size, :]
-            w = jnp.exp2((s - mu) * exp_c)
-            part = jnp.sum(w.reshape(size // 8, 8, hd), axis=0)
-            wt = w.astype(jnp.bfloat16).T
+            wt, part = weights(g, lo, size, mu)
             for r in range(0, GROUP, 2):
                 rs = slice(r * n_heads, (r + 2) * n_heads)
-                vc = jnp.concatenate([vb[g % RING, r + i, lo:lo + size, :] for i in range(2)], axis=1)
-                o = jnp.dot(wt[rs, :], vc, preferred_element_type=jnp.float32)
-                o = jnp.concatenate([o[:n_heads, :hd], o[n_heads:, hd:]], axis=0)
+                o = weighted(g, r, wt[rs, :], lo, size)
                 if lo == 0:
                     oacc[rs, :] = o
                 else:
@@ -188,34 +195,60 @@
             for d in far_first:
                 p_copy(g, d).start()
 
-        prow_i = lax.broadcasted_iota(jnp.int32, (prow, hd), 0)
-        pick = (prow_i % GROUP) * n_heads + prow_i // GROUP
-        lane_p = lax.broadcasted_iota(jnp.int32, (prow, hd), 1)
-        picked = [lane_p == pick + d * heads_local for d in range(4)]
-
-        def to_col(d, row):
-            return jnp.sum(jnp.where(picked[d], row, 0.0), axis=1, keepdims=True)
-
-        def combine(g):
-            parts = [prec[g, d] for d in range(3)] + [psend[3, g]]
-            rs = slice(g * GROUP, (g + 1) * GROUP)
+        def t_copy(c, d):
+            return pltpu.make_async_remote_copy(
+                src_ref=tsend.at[d, c], dst_ref=trec.at[c, d], send_sem=ts_sem.at[d],
+                recv_sem=tr_sem.at[c], device_id=(bx, peers[d]), device_id_type=MESH)
+
+        def send_piece(c, l_row):
+            ml = jnp.where(sub == 0, mrow[last % 2], jnp.where(sub == 1, l_row, 0.0))
+            for h in range(n_heads):
+                k, hh = h // heads_local, h % heads_local
+                tsend[k, c, hh * PIECE:(hh + 1) * PIECE, :] = (
+                    oacc[pl.ds(c * PIECE * n_heads + h, PIECE, stride=n_heads), :])
+            for k in range(4):
+                tsend[k, c, piece_rows:piece_rows + 8, :] = ml
+            for d in far_first:
+                t_copy(c, d).start()
+
+        def picks(nr, r0):
+            row = lax.broadcasted_iota(jnp.int32, (heads_local * nr, hd), 0)
+            at = (r0 + row % nr) * n_heads + row // nr
+            lane_p = lax.broadcasted_iota(jnp.int32, (heads_local * nr, hd), 1)
+            return [lane_p == at + d * heads_local for d in range(4)]
+
+        def combine_rows(parts, row0, nr, picked):
+            n = heads_local * nr
+            rs = slice(row0, row0 + nr)
+
+            def to_col(d, row):
+                return jnp.sum(jnp.where(picked[d], row, 0.0), axis=1, keepdims=True)
+
             s_new = jnp.concatenate([snew[h, rs, :] for h in range(heads_local)], axis=0)
-            ms = [to_col(d, p[prow:prow + 1, :]) for d, p in enumerate(parts)]
-            ls = [to_col(d, p[prow + 1:prow + 2, :]) for d, p in enumerate(parts)]
+            ms = [to_col(d, p[n:n + 1, :]) for d, p in enumerate(parts)]
+            ls = [to_col(d, p[n + 1:n + 2, :]) for d, p in enumerate(parts)]
             top = s_new
             for m in ms:
                 top = jnp.maximum(top, m)
             f_new = jnp.exp2((s_new - top) * exp_c)
             den = f_new
-            v_rows = vnf[rs, :]
-            num = f_new * jnp.concatenate([v_rows] * heads_local, axis=0)
+            num = f_new * jnp.concatenate([vnf[rs, :]] * heads_local, axis=0)
             for p, m, l in zip(parts, ms, ls):
                 f = jnp.exp2((m - top) * exp_c)
                 den = den + f * l
-                num = num + f * p[:prow, :]
+                num = num + f * p[:n, :]
             o = num / den
             for h in range(heads_local):
-                attn[rs, h * hd:(h + 1) * hd] = o[h * GROUP:(h + 1) * GROUP, :]
+                attn[rs, h * hd:(h + 1) * hd] = o[h * nr:(h + 1) * nr, :]
+
+        def combine(g):
+            parts = [prec[g, d] for d in range(3)] + [psend[3, g]]
+            combine_rows(parts, g * GROUP, GROUP, picks(GROUP, 0))
+
+        def combine_piece(c):
+            pltpu.make_async_copy(trec.at[c], trec.at[c], tr_sem.at[c]).wait()
+            parts = [trec[c, d] for d in range(3)] + [tsend[3, c]]
+            combine_rows(parts, last * GROUP + c * PIECE, PIECE, picks(PIECE, c * PIECE))
 
         def p_wait(g):
             pltpu.make_async_copy(prec.at[g], prec.at[g], pr_sem.at[g]).wait()
@@ -225,23 +258,25 @@
         def y_copy(b, g0, ng, d):
             sl = pl.ds(g0 * GROUP, ng * GROUP)
             return pltpu.make_async_remote_copy(
-                src_ref=ysend.at[peers[d], sl], dst_ref=yrec.at[d, sl], send_sem=ys_sem.at[d],
+                src_ref=ysend.at[d, sl], dst_ref=y_hbm.at[d, sl], send_sem=ys_sem.at[d],
                 recv_sem=yr_sem.at[b], device_id=(bx, peers[d]), device_id_type=MESH)
 
         def project(g0, ng):
             b = len(y_batches)
             y_batches.append((b, g0, ng))
             sl = slice(g0 * GROUP, (g0 + ng) * GROUP)
-            yp = jnp.dot(attn[sl, :].astype(jnp.bfloat16), wo[...], preferred_element_type=jnp.float32)
-            for k in range(4):
-                ysend[k, sl, :] = yp[:, k * q_cols:(k + 1) * q_cols]
-            for d in far_first:
-                y_copy(b, g0, ng, d).start()
+            lhs = attn[sl, :].astype(jnp.bfloat16)
+            for d in far_first + (3,):
+                col = pl.multiple_of((me if d == 3 else peers[d]) * q_cols, q_cols)
+                ysend[d, sl, :] = jnp.dot(lhs, wo[:, pl.ds(col, q_cols)], preferred_element_type=jnp.float32)
+                if d < 3:
+                    y_copy(b, g0, ng, d).start()
+                else:
+                    cp(ysend.at[3, sl], y_hbm.at[3, sl], out_sem.at[2]).start()
 
         def finish(b, g0, ng):
-            sl = slice(g0 * GROUP, (g0 + ng) * GROUP)
-            pltpu.make_async_copy(yrec.at[:, sl], yrec.at[:, sl], yr_sem.at[b]).wait()
-            yout[sl, :] = (ysend[me, sl, :] + yrec[0, sl, :] + yrec[1, sl, :] + yrec[2, sl, :]).astype(jnp.bfloat16)
+            sl = pl.ds(g0 * GROUP, ng * GROUP)
+            pltpu.make_async_copy(y_hbm.at[0:3, sl], y_hbm.at[0:3, sl], yr_sem.at[b]).wait()
 
         q_wait(0)
         build_q(0)
@@ -255,13 +290,13 @@
         def shift(g):
             return jnp.where(lens_row(g) > base, mrow[g % 2, 0:1, :], 0.0)
 
-        for g in range(last):
+        for g in range(last - 1):
             if g + 3 < n_groups:
                 k_copy(g + 3).start()
             if g + 2 < last:
                 v_copy(g + 2).start()
             if g + 2 == last:
-                for c in range(n_tail):
+                for c in range(n_pieces):
                     v_tail(c).start()
             q_wait(g + 1)
             if g >= 2:
@@ -285,37 +320,59 @@
             if g in Y_BATCHES:
                 project(*Y_BATCHES[g])
 
+        pre = last - 1
+        q_wait(last)
+        p_wait(pre - 2)
+        k_copy(last).wait()
+        build_q(last)
+        ln = lens_row(last)
+        m = jnp.full((8, hd), MASKED, jnp.float32)
+        for c in range(seq // CHUNK):
+            m = jnp.maximum(m, scores(last, c, ln))
+        keep_max(last, m)
+        combine(pre - 2)
+        mu = shift(pre)
+        v_copy(pre).wait()
+        l = jnp.zeros((8, hd), jnp.float32)
+        for c in range(seq // CHUNK):
+            l = l + values(pre, c * CHUNK, CHUNK, mu)
+        send_part(pre, l)
         mu = shift(last)
         l = jnp.zeros((8, hd), jnp.float32)
-        for c in range(n_tail):
+        for c in range(seq // CHUNK):
+            wt, part = weights(last, c * CHUNK, CHUNK, mu)
+            wts[:, c * CHUNK:(c + 1) * CHUNK] = wt
+            l = l + part
+        l_row = jnp.sum(l, axis=0, keepdims=True)
+        for c in range(n_pieces):
             v_tail(c).wait()
-            l = l + values(last, c * TAIL_CHUNK, TAIL_CHUNK, mu)
-        send_part(last, l)
-        p_wait(last - 2)
-        combine(last - 2)
-        p_wait(last - 1)
-        combine(last - 1)
-        project(last - 2, 2)
-        for b in y_batches[:-1]:
+            for r in range(c * PIECE, (c + 1) * PIECE, 2):
+                rs = slice(r * n_heads, (r + 2) * n_heads)
+                oacc[rs, :] = weighted(last, r, wts[rs, :], 0, seq)
+            send_piece(c, l_row)
+        p_wait(pre - 1)
+        combine(pre - 1)
+        project(pre - 2, 2)
+        p_wait(pre)
+        combine(pre)
+        project(pre, 1)
+        for c in range(n_pieces):
+            combine_piece(c)
+        project(last, 1)
+        for b in y_batches:
             finish(*b)
-        p_wait(last)
-        combine(last)
-        project(last, 1)
-        finish(*y_batches[-2])
-        finish(*y_batches[-1])
-        y_out = cp(yout, y_hbm, out_sem.at[2])
-        y_out.start()
         for d in range(3):
             pltpu.make_async_copy(qown, qown, qs_sem.at[d]).wait()
             pltpu.make_async_copy(psend.at[d], psend.at[d], ps_sem.at[d]).wait()
+            pltpu.make_async_copy(tsend.at[d], tsend.at[d], ts_sem.at[d]).wait()
             pltpu.make_async_copy(ysend.at[d], ysend.at[d], ys_sem.at[d]).wait()
         cp(kn16, kn_hbm, out_sem.at[0]).wait()
         cp(vn16, vn_hbm, out_sem.at[1]).wait()
-        y_out.wait()
+        cp(ysend.at[3], y_hbm.at[3], out_sem.at[2]).wait()
 
     f32, bf16 = jnp.float32, jnp.bfloat16
     dma = pltpu.SemaphoreType.DMA
-    n_b = len(Y_BATCHES) + 2
+    n_b = len(Y_BATCHES) + 3
     scratch = [
         pltpu.VMEM((rows, embed), bf16), pltpu.VMEM((embed, q_cols), bf16), pltpu.VMEM((2, embed, hd), bf16),
         pltpu.VMEM((q_cols, embed), bf16), pltpu.SMEM((rows,), jnp.int32),
@@ -325,25 +382,32 @@
         pltpu.VMEM((2, seq, hd), f32), pltpu.VMEM((hd, hd), f32), pltpu.VMEM((2, 8, hd), f32),
         pltpu.VMEM((rows, hd), f32),
         pltpu.VMEM((rows, hd), bf16), pltpu.VMEM((rows, hd), bf16), pltpu.VMEM((heads_local, rows, hd), f32),
-        pltpu.VMEM((4, n_groups, prow + 8, hd), f32), pltpu.VMEM((n_groups, 3, prow + 8, hd), f32),
-        pltpu.VMEM((rows, q_cols), f32), pltpu.VMEM((4, rows, q_cols), f32), pltpu.VMEM((3, rows, q_cols), f32),
-        pltpu.VMEM((rows, q_cols), bf16),
-        dma((6,)), dma((RING,)), dma((RING,)), dma((n_tail,)), dma((3,)), dma((n_groups,)),
-        dma((3,)), dma((n_groups,)), dma((3,)), dma((n_b,)), dma((3,)),
+        pltpu.VMEM((hd, seq), bf16),
+        pltpu.VMEM((4, last, prow + 8, hd), f32), pltpu.VMEM((last, 3, prow + 8, hd), f32),
+        pltpu.VMEM((4, n_pieces, piece_rows + 8, hd), f32), pltpu.VMEM((n_pieces, 3, piece_rows + 8, hd), f32),
+        pltpu.VMEM((rows, q_cols), f32), pltpu.VMEM((4, rows, q_cols), f32),
+        dma((6,)), dma((RING,)), dma((RING,)), dma((n_pieces,)), dma((3,)), dma((n_groups,)),
+        dma((3,)), dma((last,)), dma((3,)), dma((n_pieces,)), dma((3,)), dma((n_b,)), dma((3,)),
     ]
     return kernel, scratch
 
 
-def store_kernel(y_ref, k_ref, v_ref, yo_ref, ko_ref, vo_ref, y_buf, k_buf, v_buf, sem):
-    trips = [(y_ref, y_buf, yo_ref), (k_ref, k_buf, ko_ref), (v_ref, v_buf, vo_ref)]
+def store_kernel(y_ref, k_ref, v_ref, yo_ref, ko_ref, vo_ref, y_buf, y16, k_buf, v_buf, sem):
+    trips = [(k_ref, k_buf, ko_ref), (v_ref, v_buf, vo_ref)]
+    y_in = pltpu.make_async_copy(y_ref, y_buf, sem.at[4])
+    y_in.start()
     reads = [pltpu.make_async_copy(a, b, sem.at[i]) for i, (a, b, _) in enumerate(trips)]
-    writes = [pltpu.make_async_copy(b, c, sem.at[3 + i]) for i, (_, b, c) in enumerate(trips)]
+    writes = [pltpu.make_async_copy(b, c, sem.at[2 + i]) for i, (_, b, c) in enumerate(trips)]
     for c in reads:
         c.start()
     for r, w in zip(reads, writes):
         r.wait()
         w.start()
-    for w in writes:
+    y_in.wait()
+    y16[...] = (y_buf[3] + y_buf[0] + y_buf[1] + y_buf[2]).astype(y16.dtype)
+    y_w = pltpu.make_async_copy(y16, yo_ref, sem.at[5])
+    y_w.start()
+    for w in writes + [y_w]:
         w.wait()
 
 
@@ -361,7 +425,7 @@
                 jax.ShapeDtypeStruct((rows, hd), jnp.bfloat16))
         raw = pl.pallas_call(
             kernel,
-            out_shape=outs,
+            out_shape=(jax.ShapeDtypeStruct((4, rows, q_cols), jnp.float32),) + outs[1:],
             in_specs=[any_spec] * 8,
             out_specs=(any_spec,) * 3,
             scratch_shapes=scratch,
@@ -374,7 +438,8 @@
             out_shape=outs,
             in_specs=[any_spec] * 3,
             out_specs=(any_spec,) * 3,
-            scratch_shapes=[pltpu.VMEM(o.shape, o.dtype) for o in outs] + [pltpu.SemaphoreType.DMA((6,))],
+            scratch_shapes=[pltpu.VMEM((4, rows, q_cols), jnp.float32)] + [pltpu.VMEM(o.shape, o.dtype) for o in outs]
+            + [pltpu.SemaphoreType.DMA((6,))],
             name="store_outputs",
         )(*raw)
 

time: 36.4 us -> 36.1 us (level)
    pallas_call x1, Pallas kernels: 33.9 us -> 33.5 us  [local_step(): pl.pallas_call(kernel, out_shape=(jax.ShapeDtypeStruct((4, rows, q_cols),...]
where the time goes in v3:
time: 36.1 us; the launch traced here: 36 us
  Pallas kernels  35.2 us (98%)
  between operations  0.8 us (2%)
    pallas_call x1, Pallas kernels, local_step(): pl.pallas_call(kernel, out_shape=(jax.ShapeDtypeStruct((4, rows, q_cols),...  33.5 us
    pallas_call x1, Pallas kernels, local_step(): pl.pallas_call(store_kernel, out_shape=outs, in_specs=[any_spec] * 3, out...  1.75 us

profile of v3, /device:TPU:0, one launch (start us, length us, event | category | flops | bytes accessed | tf_op | source)
XLA Modules:
  0.0 36.0 jit_solution(16701289811426323013)
XLA Ops:
  0.6 33.5 %mqa_decode.1 = (f32[4,64,512]{2,1,0:T(8,128)}, bf16[64,128]{1,0:T(8,128)(2,1)}, bf16[64,128]{1,0:T(8,128)(2,1)}) custom-call(bf16[64,2048]{1,0:T(8,128)(2,1)} %hid_hbm.1, bf16[2048,512]{1,0:T(8,128)(2,1)} %wq_hbm.1, bf16[2048,128]{1,0:T(8,128)(2,1)} %wk_hbm.1, bf16[2048,128]{1,0:T(8,128)(2,1)} %wv_hbm.1, bf16[512,2048]{1,0:T(8,128)(2,1)} %wo_hbm.1, ...), custom_call_target="tpu_custom_call" | custom-call | tf_op jit(solution)/shard_map/mqa_decode/pallas_call | solution.py:426
  34.1 1.8 %store_outputs.1 = (bf16[64,512]{1,0:T(8,128)(2,1)}, bf16[64,128]{1,0:T(8,128)(2,1)}, bf16[64,128]{1,0:T(8,128)(2,1)}) custom-call(f32[4,64,512]{2,1,0:T(8,128)} %get-tuple-element.6.y_ref, bf16[64,128]{1,0:T(8,128)(2,1)} %get-tuple-element.7.k_ref, bf16[64,128]{1,0:T(8,128)(2,1)} %get-tuple-element.8.v_ref), custom_call_target="tpu_custom_call" | custom-call | tf_op jit(solution)/shard_map/store_outputs/pallas_call | solution.py:436

commit v4 on v3

--- a/solution.py
+++ b/solution.py
@@ -13,7 +13,7 @@
 PIECE = 4
 MASKED = -3e38
 MESH = pl.DeviceIdType.MESH
-Y_BATCHES = {3: (0, 2), 5: (2, 2)}
+Y_BATCHES = {5: (0, 4)}
 
 
 def make_kernel(rows, embed, seq, heads_local, hd):
@@ -30,11 +30,10 @@
     prow = heads_local * GROUP
 
     def kernel(hid_hbm, wq_hbm, wk_hbm, wv_hbm, wo_hbm, k_hbm, v_hbm, len_hbm,
-               y_hbm, kn_hbm, vn_hbm,
+               y_out, kn_out, vn_out,
                hid, wq, wkv, wo, lens_s, kb, vb, qown, qrec, qmat, qblk, sbuf, oacc, mrow,
-               vnf, kn16, vn16, snew, wts, psend, prec, tsend, trec, attn, ysend,
-               in_sem, ksem, vsem, tsem, qs_sem, qr_sem, ps_sem, pr_sem, ts_sem, tr_sem, ys_sem, yr_sem,
-               out_sem):
+               vnf, snew, wts, psend, prec, tsend, trec, attn, ysend,
+               in_sem, ksem, vsem, tsem, qs_sem, qr_sem, ps_sem, pr_sem, ts_sem, tr_sem, ys_sem, yr_sem):
         bx = lax.axis_index('bx')
         me = lax.axis_index('sq')
         chip, core = me // 2, me % 2
@@ -114,10 +113,8 @@
         ins[4].wait()
         kn = rope(jnp.dot(hid[...], wkv[0], preferred_element_type=jnp.float32)).astype(jnp.bfloat16)
         vn = jnp.dot(hid[...], wkv[1], preferred_element_type=jnp.float32).astype(jnp.bfloat16)
-        kn16[...] = kn
-        vn16[...] = vn
-        cp(kn16, kn_hbm, out_sem.at[0]).start()
-        cp(vn16, vn_hbm, out_sem.at[1]).start()
+        kn_out[...] = kn
+        vn_out[...] = vn
         knf = kn.astype(jnp.float32)
         vnf[...] = vn.astype(jnp.float32)
         for h in range(heads_local):
@@ -258,7 +255,7 @@
         def y_copy(b, g0, ng, d):
             sl = pl.ds(g0 * GROUP, ng * GROUP)
             return pltpu.make_async_remote_copy(
-                src_ref=ysend.at[d, sl], dst_ref=y_hbm.at[d, sl], send_sem=ys_sem.at[d],
+                src_ref=ysend.at[d, sl], dst_ref=y_out.at[d, sl], send_sem=ys_sem.at[d],
                 recv_sem=yr_sem.at[b], device_id=(bx, peers[d]), device_id_type=MESH)
 
         def project(g0, ng):
@@ -268,15 +265,16 @@
             lhs = attn[sl, :].astype(jnp.bfloat16)
             for d in far_first + (3,):
                 col = pl.multiple_of((me if d == 3 else peers[d]) * q_cols, q_cols)
-                ysend[d, sl, :] = jnp.dot(lhs, wo[:, pl.ds(col, q_cols)], preferred_element_type=jnp.float32)
+                yp = jnp.dot(lhs, wo[:, pl.ds(col, q_cols)], preferred_element_type=jnp.float32)
                 if d < 3:
+                    ysend[d, sl, :] = yp
                     y_copy(b, g0, ng, d).start()
                 else:
-                    cp(ysend.at[3, sl], y_hbm.at[3, sl], out_sem.at[2]).start()
+                    y_out[3, sl, :] = yp
 
         def finish(b, g0, ng):
             sl = pl.ds(g0 * GROUP, ng * GROUP)
-            pltpu.make_async_copy(y_hbm.at[0:3, sl], y_hbm.at[0:3, sl], yr_sem.at[b]).wait()
+            pltpu.make_async_copy(y_out.at[0:3, sl], y_out.at[0:3, sl], yr_sem.at[b]).wait()
 
         q_wait(0)
         build_q(0)
@@ -366,9 +364,6 @@
             pltpu.make_async_copy(psend.at[d], psend.at[d], ps_sem.at[d]).wait()
             pltpu.make_async_copy(tsend.at[d], tsend.at[d], ts_sem.at[d]).wait()
             pltpu.make_async_copy(ysend.at[d], ysend.at[d], ys_sem.at[d]).wait()
-        cp(kn16, kn_hbm, out_sem.at[0]).wait()
-        cp(vn16, vn_hbm, out_sem.at[1]).wait()
-        cp(ysend.at[3], y_hbm.at[3], out_sem.at[2]).wait()
 
     f32, bf16 = jnp.float32, jnp.bfloat16
     dma = pltpu.SemaphoreType.DMA
@@ -381,33 +376,24 @@
         pltpu.VMEM((hd, hd), f32), pltpu.VMEM((GROUP * hd, hd), bf16),
         pltpu.VMEM((2, seq, hd), f32), pltpu.VMEM((hd, hd), f32), pltpu.VMEM((2, 8, hd), f32),
         pltpu.VMEM((rows, hd), f32),
-        pltpu.VMEM((rows, hd), bf16), pltpu.VMEM((rows, hd), bf16), pltpu.VMEM((heads_local, rows, hd), f32),
+        pltpu.VMEM((heads_local, rows, hd), f32),
         pltpu.VMEM((hd, seq), bf16),
         pltpu.VMEM((4, last, prow + 8, hd), f32), pltpu.VMEM((last, 3, prow + 8, hd), f32),
         pltpu.VMEM((4, n_pieces, piece_rows + 8, hd), f32), pltpu.VMEM((n_pieces, 3, piece_rows + 8, hd), f32),
-        pltpu.VMEM((rows, q_cols), f32), pltpu.VMEM((4, rows, q_cols), f32),
+        pltpu.VMEM((rows, q_cols), f32), pltpu.VMEM((3, rows, q_cols), f32),
         dma((6,)), dma((RING,)), dma((RING,)), dma((n_pieces,)), dma((3,)), dma((n_groups,)),
-        dma((3,)), dma((last,)), dma((3,)), dma((n_pieces,)), dma((3,)), dma((n_b,)), dma((3,)),
+        dma((3,)), dma((last,)), dma((3,)), dma((n_pieces,)), dma((3,)), dma((n_b,)),
     ]
     return kernel, scratch
 
 
-def store_kernel(y_ref, k_ref, v_ref, yo_ref, ko_ref, vo_ref, y_buf, y16, k_buf, v_buf, sem):
-    trips = [(k_ref, k_buf, ko_ref), (v_ref, v_buf, vo_ref)]
-    y_in = pltpu.make_async_copy(y_ref, y_buf, sem.at[4])
-    y_in.start()
-    reads = [pltpu.make_async_copy(a, b, sem.at[i]) for i, (a, b, _) in enumerate(trips)]
-    writes = [pltpu.make_async_copy(b, c, sem.at[2 + i]) for i, (_, b, c) in enumerate(trips)]
-    for c in reads:
-        c.start()
-    for r, w in zip(reads, writes):
-        r.wait()
+def store_kernel(y_ref, k_ref, v_ref, yo_ref, ko_ref, vo_ref, y16, sem):
+    y16[...] = (y_ref[3] + y_ref[0] + y_ref[1] + y_ref[2]).astype(y16.dtype)
+    writes = [pltpu.make_async_copy(a, b, sem.at[i])
+              for i, (a, b) in enumerate(((y16, yo_ref), (k_ref, ko_ref), (v_ref, vo_ref)))]
+    for w in writes:
         w.start()
-    y_in.wait()
-    y16[...] = (y_buf[3] + y_buf[0] + y_buf[1] + y_buf[2]).astype(y16.dtype)
-    y_w = pltpu.make_async_copy(y16, yo_ref, sem.at[5])
-    y_w.start()
-    for w in writes + [y_w]:
+    for w in writes:
         w.wait()
 
 
@@ -420,28 +406,29 @@
         q_cols = heads_local * hd
         kernel, scratch = make_kernel(rows, embed, seq, heads_local, hd)
         any_spec = pl.BlockSpec(memory_space=pl.ANY)
+        vmem_spec = pl.BlockSpec(memory_space=pltpu.VMEM)
         outs = (jax.ShapeDtypeStruct((rows, q_cols), jnp.bfloat16),
                 jax.ShapeDtypeStruct((rows, hd), jnp.bfloat16),
                 jax.ShapeDtypeStruct((rows, hd), jnp.bfloat16))
         raw = pl.pallas_call(
             kernel,
-            out_shape=(jax.ShapeDtypeStruct((4, rows, q_cols), jnp.float32),) + outs[1:],
+            out_shape=tuple(pltpu.VMEM(sh, dt) for sh, dt in (((4, rows, q_cols), jnp.float32),
+                                                              ((rows, hd), jnp.bfloat16), ((rows, hd), jnp.bfloat16))),
             in_specs=[any_spec] * 8,
-            out_specs=(any_spec,) * 3,
+            out_specs=(vmem_spec,) * 3,
             scratch_shapes=scratch,
             compiler_params=pltpu.CompilerParams(
-                collective_id=0, has_side_effects=True, vmem_limit_bytes=67043328),
+                collective_id=0, has_side_effects=True, vmem_limit_bytes=66300000),
             name="mqa_decode",
         )(hidden, w_query, w_key, w_value, w_out, k_cache, v_cache, lengths)
         return pl.pallas_call(
             store_kernel,
             out_shape=outs,
-            in_specs=[any_spec] * 3,
+            in_specs=[vmem_spec] * 3,
             out_specs=(any_spec,) * 3,
-            scratch_shapes=[pltpu.VMEM((4, rows, q_cols), jnp.float32)] + [pltpu.VMEM(o.shape, o.dtype) for o in outs]
-            + [pltpu.SemaphoreType.DMA((6,))],
+            scratch_shapes=[pltpu.VMEM(outs[0].shape, outs[0].dtype), pltpu.SemaphoreType.DMA((3,))],
             name="store_outputs",
-        )(*raw)
+        )(*[pltpu.with_memory_space_constraint(r, pltpu.VMEM) for r in raw])
 
     return jax.shard_map(
         local_step,

time: 36.1 us -> 35.3 us (0.978)
  Pallas kernels: 35.2 us -> 34.4 us
    pallas_call x2, Pallas kernels: 35.2 us -> 34.4 us  [the longest x1 33.8 us: local_step(): pl.pallas_call(kernel, out_shape=tuple((pltpu.VMEM(sh, dt) for sh, dt in...]
where the time goes in v4:
time: 35.3 us; the launch traced here: 35.2 us
  Pallas kernels  34.4 us (97%)
  between operations  0.8 us (2%)
    pallas_call x1, Pallas kernels, local_step(): pl.pallas_call(kernel, out_shape=tuple((pltpu.VMEM(sh, dt) for sh, dt in...  33.8 us

profile of v4, /device:TPU:0, one launch (start us, length us, event | category | flops | bytes accessed | tf_op | source)
XLA Modules:
  0.0 35.2 jit_solution(4582382754612116157)
XLA Ops:
  0.6 33.8 %mqa_decode.1 = (f32[4,64,512]{2,1,0:T(8,128)S(1)}, bf16[64,128]{1,0:T(8,128)(2,1)S(1)}, bf16[64,128]{1,0:T(8,128)(2,1)S(1)}) custom-call(bf16[64,2048]{1,0:T(8,128)(2,1)} %hid_hbm.1, bf16[2048,512]{1,0:T(8,128)(2,1)} %wq_hbm.1, bf16[2048,128]{1,0:T(8,128)(2,1)} %wk_hbm.1, bf16[2048,128]{1,0:T(8,128)(2,1)} %wv_hbm.1, bf16[512,2048]{1,0:T(8,128)(2,1)} %wo_hbm.1, ...), custom_call_target="tpu_custom_call" | custom-call | tf_op jit(solution)/shard_map/mqa_decode/pallas_call | solution.py:413
  34.4 0.7 %store_outputs.1 = (bf16[64,512]{1,0:T(8,128)(2,1)}, bf16[64,128]{1,0:T(8,128)(2,1)}, bf16[64,128]{1,0:T(8,128)(2,1)}) custom-call(f32[4,64,512]{2,1,0:T(8,128)S(1)} %get-tuple-element.6.y_ref, bf16[64,128]{1,0:T(8,128)(2,1)S(1)} %get-tuple-element.7.k_ref, bf16[64,128]{1,0:T(8,128)(2,1)S(1)} %get-tuple-element.8.v_ref), custom_call_target="tpu_custom_call" | custom-call | tf_op jit(solution)/shard_map/store_outputs/pallas_call | solution.py:424
